TPU v7x, 32 devices: a whole 2x2x4 slice. The times are simulated.
32 devices in a mesh: img: 8 (over z, core), txt: 4 (over y, x).
Axes of the slice: x: 2, y: 2, z: 4, core: 2. Of those that a mesh axis runs over, the one named last changes fastest.
Arguments:
- teacher_img: bfloat16 [8192, 1280], P('img'), may hold values from -40 to 40
- teacher_txt: bfloat16 [4096, 1280], P('txt'), may hold values from -40 to 40
- student_img: bfloat16 [8192, 512], P('img'), may hold values from -40 to 40
- student_txt: bfloat16 [4096, 512], P('txt'), may hold values from -40 to 40
Outputs:
- loss: float32 [], replicated
- grad_img: float32 [8192, 512], P(('img', 'txt'))
- grad_txt: float32 [4096, 512], P(('txt', 'img'))
All inputs are finite; a program needn't handle non-finite values.
Results may differ from a plain program's by a relative error of at most 0.0033.
Values sent between devices are 32-bit elements; how exact they have to be, the bound alone decides.
A program may use at most 64 MiB of HBM per device.

v0:
```python
import math
import jax
import jax.numpy as jnp
from jax import lax
from jax.sharding import PartitionSpec as P


def body(teacher_img, teacher_txt, student_img, student_txt):
    scale_teach = 3.0 / math.sqrt(teacher_img.shape[1])
    scale_learn = 3.0 / math.sqrt(student_img.shape[1])
    rows = teacher_img.shape[0]
    cols = teacher_txt.shape[0]
    img_count = lax.axis_size("img")
    txt_count = lax.axis_size("txt")
    teacher = scale_teach * jnp.einsum(
        "id,jd->ij", teacher_img, teacher_txt, preferred_element_type=jnp.float32
    )
    student = scale_learn * jnp.einsum(
        "id,jd->ij", student_img, student_txt, preferred_element_type=jnp.float32
    )
    row_tpeak, row_lpeak = lax.pmax((jnp.max(teacher, axis=1), jnp.max(student, axis=1)), "txt")
    col_tpeak, col_lpeak = lax.pmax((jnp.max(teacher, axis=0), jnp.max(student, axis=0)), "img")
    row_tmass, row_lmass = lax.psum(
        (
            jnp.sum(jnp.exp(teacher - row_tpeak[:, None]), axis=1),
            jnp.sum(jnp.exp(student - row_lpeak[:, None]), axis=1),
        ),
        "txt",
    )
    col_tmass, col_lmass = lax.psum(
        (
            jnp.sum(jnp.exp(teacher - col_tpeak[None, :]), axis=0),
            jnp.sum(jnp.exp(student - col_lpeak[None, :]), axis=0),
        ),
        "img",
    )
    row_teach = row_tpeak + jnp.log(row_tmass)
    row_learn = row_lpeak + jnp.log(row_lmass)
    col_teach = col_tpeak + jnp.log(col_tmass)
    col_learn = col_lpeak + jnp.log(col_lmass)
    p_row = jnp.exp(teacher - row_teach[:, None])
    q_row = jnp.exp(student - row_learn[:, None])
    p_col = jnp.exp(teacher - col_teach[None, :])
    q_col = jnp.exp(student - col_learn[None, :])
    gap = teacher - student
    row_part = (jnp.sum(p_row * gap) + jnp.sum(row_learn - row_teach) / txt_count) / (
        rows * img_count
    )
    col_part = (jnp.sum(p_col * gap) + jnp.sum(col_learn - col_teach) / img_count) / (
        cols * txt_count
    )
    delta = (8.0 * (q_row - p_row + q_col - p_col)).astype(jnp.bfloat16)
    loss = 0.5 * lax.psum(row_part + col_part, ("img", "txt"))
    picked = delta
    grad_txt = lax.psum_scatter(
        scale_learn
        * jnp.einsum("ij,id->jd", picked, student_img, preferred_element_type=jnp.float32),
        "img",
        scatter_dimension=0,
        tiled=True,
    )
    picked = delta
    grad_img = lax.psum_scatter(
        scale_learn * jnp.dot(picked, student_txt, preferred_element_type=jnp.float32),
        "txt",
        scatter_dimension=0,
        tiled=True,
    )
    return (loss, grad_img, grad_txt)


def solution(mesh):
    placed = (P("img", None), P("txt", None), P("img", None), P("txt", None))
    return jax.shard_map(
        body,
        mesh=mesh,
        in_specs=placed,
        out_specs=(P(), P(("img", "txt"), None), P(("txt", "img"), None)),
        check_vma=False,
    )
```

profile of v0, /device:TPU:0, one launch (start us, length us, event | category | flops | bytes accessed | tf_op | source)
XLA Modules:
  0.0 193.4 jit_solution(10971360036748988000)
XLA Ops:
  7.2 0.0 copy-start
  7.2 0.0 reduce-scatter.3.cloned.1.call-start
  7.2 1.7 copy-done
  8.9 0.0 copy-start.2
  8.9 0.0 copy-start.4
  8.9 6.4 %multiply_reduce_fusion.4 = (f32[1024]{0:T(1024)S(1)}, f32[1024]{0:T(1024)S(1)}, f32[1024,1024]{1,0:T(8,128)}) fusion(bf16[1024,1280]{1,0:T(8,128)(2,1)S(1)} %copy-done, bf16[1024,1280]{1,0:T(8,128)(2,1)} %param.5), kind=kOutput, calls=%fused_computation.12 | convolution fusion | flops 2687498240 | bytes 9445376 | tf_op jit(solution)/shard_map/id,jd->ij/dot_general | solution.py:15
  15.3 0.0 copy-done.2
  15.3 0.0 copy-done.4
  15.3 3.2 %multiply_reduce_fusion.2 = (f32[1024]{0:T(1024)S(1)}, f32[1024]{0:T(1024)S(1)}, f32[1024,1024]{1,0:T(8,128)}) fusion(bf16[1024,512]{1,0:T(8,128)(2,1)S(1)} %copy-done.4, bf16[1024,512]{1,0:T(8,128)(2,1)S(1)} %copy-done.2), kind=kOutput, calls=%fused_computation.9 | convolution fusion | flops 1076885504 | bytes 6299648 | tf_op jit(solution)/shard_map/id,jd->ij/dot_general | solution.py:18
  18.5 18.3 %all-reduce = (f32[1024]{0:T(1024)S(1)}, f32[1024]{0:T(1024)S(1)}) all-reduce(f32[1024]{0:T(1024)S(1)} %get-tuple-element.11, f32[1024]{0:T(1024)S(1)} %get-tuple-element.6), channel_id=1, replica_groups=mesh['img'=8,'txt'=4] {'img'}, use_global_device_ids=true, to_apply=%region_11.0 | all-reduce | flops 2048 | bytes 16384 | tf_op jit(solution)/shard_map/pmax | solution.py:22
  36.9 10.1 %all-reduce.1 = (f32[1024]{0:T(1024)S(1)}, f32[1024]{0:T(1024)S(1)}) all-reduce(f32[1024]{0:T(1024)S(1)} %get-tuple-element.12, f32[1024]{0:T(1024)S(1)} %get-tuple-element.7), channel_id=1, replica_groups=mesh['img'=8,'txt'=4] {'txt'}, use_global_device_ids=true, to_apply=%region_1.0 | all-reduce | flops 2048 | bytes 16384 | tf_op jit(solution)/shard_map/pmax | solution.py:21
  47.0 3.7 %exponential_reduce_fusion.1 = (f32[1024]{0:T(1024)S(1)}, f32[1024]{0:T(1024)S(1)}) fusion(f32[1024,1024]{1,0:T(8,128)} %get-tuple-element.21, f32[1024]{0:T(1024)S(1)} %get-tuple-element.13, f32[1024]{0:T(1024)S(1)} %get-tuple-element.15), kind=kLoop, calls=%fused_computation.4 | loop fusion | flops 5240832 | bytes 4210688 | tf_op jit(solution)/shard_map/reduce_sum | solution.py:32
  50.7 13.6 %psum.37 = f32[1024]{0:T(1024)S(1)} all-reduce(f32[1024]{0:T(1024)S(1)} %get-tuple-element.9), channel_id=1, replica_groups=mesh['img'=8,'txt'=4] {'img'}, use_global_device_ids=true, to_apply=%region_13.0 | all-reduce | flops 1024 | bytes 8192 | tf_op jit(solution)/shard_map/psum | solution.py:30
  64.3 7.9 %psum.35 = f32[1024]{0:T(1024)S(1)} all-reduce(f32[1024]{0:T(1024)S(1)} %get-tuple-element.10), channel_id=1, replica_groups=mesh['img'=8,'txt'=4] {'txt'}, use_global_device_ids=true, to_apply=%region_3.0 | all-reduce | flops 1024 | bytes 8192 | tf_op jit(solution)/shard_map/psum | solution.py:23
  72.2 8.1 %multiply_reduce_fusion = (f32[]{:T(128)}, f32[]{:T(128)}, f32[1024]{0:T(1024)S(1)}, f32[1024]{0:T(1024)S(1)}) fusion(f32[1024,1024]{1,0:T(8,128)} %get-tuple-element.22, f32[1024,1024]{1,0:T(8,128)} %get-tuple-element.21, f32[1024]{0:T(1024)S(1)} %log_add_fusion.1, f32[1024]{0:T(1024)S(1)} %log_add_fusion.3, f32[1024]{0:T(1024)S(1)} %get-tuple-element.14, ...), kind=kLoop, calls=%fused_computation.2 | loop fusion | flops 13629438 | bytes 8413192 | tf_op jit(solution)/shard_map/reduce_sum | solution.py:49
  80.4 13.6 %psum.38 = f32[1024]{0:T(1024)S(1)} all-reduce(f32[1024]{0:T(1024)S(1)} %get-tuple-element.5), channel_id=1, replica_groups=mesh['img'=8,'txt'=4] {'img'}, use_global_device_ids=true, to_apply=%region_18.0 | all-reduce | flops 1024 | bytes 8192 | tf_op jit(solution)/shard_map/psum | solution.py:30
  93.9 0.6 subtract_reduce_fusion
  94.5 9.0 %psum.36 = f32[1024]{0:T(1024)S(1)} all-reduce(f32[1024]{0:T(1024)S(1)} %get-tuple-element.8), channel_id=1, replica_groups=mesh['img'=8,'txt'=4] {'txt'}, use_global_device_ids=true, to_apply=%region_8.0 | all-reduce | flops 1024 | bytes 8192 | tf_op jit(solution)/shard_map/psum | solution.py:23
  103.5 0.6 subtract_reduce_fusion.1
  104.2 0.0 copy-start.3
  104.2 5.1 %multiply_convert_fusion = bf16[1024,1024]{1,0:T(8,128)(2,1)S(1)} fusion(f32[1024,1024]{1,0:T(8,128)} %get-tuple-element.22, f32[1024,1024]{1,0:T(8,128)} %get-tuple-element.21, f32[1024]{0:T(1024)S(1)} %get-tuple-element.18, f32[1024]{0:T(1024)S(1)} %get-tuple-element.20, f32[1024]{0:T(1024)S(1)} %log_add_fusion.1, f32[1024]{0:T(1024)S(1)} %log_add_fusion.3), kind=kLoop, calls=%fused_computation | loop fusion | flops 11534336 | bytes 10502144 | tf_op jit(solution)/shard_map/convert_element_type | solution.py:52
  109.2 0.0 copy-start.1
  109.2 1.3 copy-done.1
  110.6 0.0 copy-done.3
  110.6 2.6 %convolution_multiply_fusion.1 = f32[1024,512]{1,0:T(8,128)} fusion(bf16[1024,1024]{1,0:T(8,128)(2,1)S(1)} %multiply_convert_fusion, bf16[1024,512]{1,0:T(8,128)(2,1)S(1)} %copy-done.3), kind=kOutput, calls=%fused_computation.15 | convolution fusion | flops 1074266112 | bytes 5242880 | tf_op jit(solution)/shard_map/dot_general | solution.py:64
  113.2 0.0 reduce-scatter.3.cloned.1.call-update
  113.2 0.0 reduce-scatter.5.cloned.1.call-start
  113.2 4.4 %convolution_multiply_fusion = f32[1024,512]{1,0:T(8,128)} fusion(bf16[1024,1024]{1,0:T(8,128)(2,1)} %copy-done.1, bf16[1024,512]{1,0:T(8,128)(2,1)} %param.6), kind=kOutput, calls=%fused_computation.14 | convolution fusion | flops 1074266112 | bytes 5242880 | tf_op jit(solution)/shard_map/ij,id->jd/dot_general | solution.py:57
  117.7 0.0 reduce-scatter.5.cloned.1.call-update
  120.1 37.2 %psum.39 = f32[]{:T(128)} all-reduce(f32[]{:T(128)S(6)} %add.44), channel_id=1, replica_groups=mesh['img'=8,'txt'=4] {'img','txt'}, use_global_device_ids=true, to_apply=%region_20.0 | all-reduce | flops 1 | bytes 8 | tf_op jit(solution)/shard_map/psum | solution.py:53
  158.0 0.0 reduce-scatter.3.cloned.1.call-done
  158.0 27.5 %reduce-scatter.5.cloned.1.call-done = f32[128,512]{1,0:T(8,128)} async-done(((f32[1024,512]{1,0:T(8,128)}), f32[128,512]{1,0:T(8,128)}) %reduce-scatter.5.cloned.1.call-update) | async-done | bytes 262160 | tf_op jit(solution)/shard_map/reduce_scatter | solution.py:55
  (2 shorter events, 0.0 us)
Async XLA Ops:
  7.2 1.7 copy-start
  7.2 150.8 %reduce-scatter.3.cloned.1.call-start = ((), (), s32[]{:S(2)}) async-start(), calls=%async_computation.2 | async-start | bytes 2621440 | tf_op jit(solution)/shard_map/reduce_scatter | solution.py:63
  8.9 6.4 %copy-start.2 = (bf16[1024,512]{1,0:T(8,128)(2,1)S(1)}, bf16[1024,512]{1,0:T(8,128)(2,1)}, u32[]{:S(2)}) copy-start(bf16[1024,512]{1,0:T(8,128)(2,1)} %param.7) | copy-start | bytes 3145732
  8.9 6.4 %copy-start.4 = (bf16[1024,512]{1,0:T(8,128)(2,1)S(1)}, bf16[1024,512]{1,0:T(8,128)(2,1)}, u32[]{:S(2)}) copy-start(bf16[1024,512]{1,0:T(8,128)(2,1)} %param.6) | copy-start | bytes 3145732
  104.2 6.4 %copy-start.3 = (bf16[1024,512]{1,0:T(8,128)(2,1)S(1)}, bf16[1024,512]{1,0:T(8,128)(2,1)}, u32[]{:S(2)}) copy-start(bf16[1024,512]{1,0:T(8,128)(2,1)} %param.7) | copy-start | bytes 3145732
  109.2 1.3 copy-start.1
  113.2 72.3 %reduce-scatter.5.cloned.1.call-start = ((), (), s32[]{:S(2)}) async-start(), calls=%async_computation.3 | async-start | bytes 2359296 | tf_op jit(solution)/shard_map/reduce_scatter | solution.py:55
Sparse Core Ops, SparseCore 0:
  113.3 33.0 reduce-scatter.2
  149.3 36.1 reduce-scatter.4
where the time goes:
time: 194 us; the launch traced here: 193 us
  blocking collectives  110 us (57%)
  waiting for transfers between devices  27.5 us (14%)
  between operations  18.3 us (9%)
  other arithmetic  18.2 us (9%)
  matrix products  16.7 us (9%)
  local copies, waits for them, and re-layouts  3.03 us (2%)
    psum x1, blocking collectives, body(): loss = 0.5 * lax.psum(row_part + col_part, ('img', 'txt'))  37.2 us
    reduce_scatter x1, waiting for transfers between devices, body(): lax.psum_scatter(scale_learn * jnp.einsum('ij,id->jd', picked, student_im...  27.5 us
    psum x2, blocking collectives, body(): lax.psum((jnp.sum(jnp.exp(teacher - col_tpeak[None, :]), axis=0), jnp.sum...  27.2 us
    pmax x1, blocking collectives, body(): lax.pmax((jnp.max(teacher, axis=0), jnp.max(student, axis=0)), 'img')  18.3 us
    psum x2, blocking collectives, body(): lax.psum((jnp.sum(jnp.exp(teacher - row_tpeak[:, None]), axis=1), jnp.sum...  16.9 us
    pmax x1, blocking collectives, body(): lax.pmax((jnp.max(teacher, axis=1), jnp.max(student, axis=1)), 'txt')  10.1 us
    reduce_sum x1, other arithmetic, body(): jnp.sum(p_col * gap) + jnp.sum(col_learn - col_teach) / img_count  8.12 us
    dot_general x1, matrix products, body(): jnp.einsum('id,jd->ij', teacher_img, teacher_txt, preferred_element_type=...  6.41 us
  transfers between devices with their start and end apart: 2, of which 1 were waited for; matrix products, arithmetic and copies ran while one was open for 2% of the time, Pallas kernels for 0%

commit v1 on v0

--- a/solution.py
+++ b/solution.py
@@ -3,6 +3,11 @@
 import jax.numpy as jnp
 from jax import lax
 from jax.sharding import PartitionSpec as P
+
+
+def one_after_other(x, axis_one, axis_two):
+    half = lax.psum(x, axis_one)
+    return lax.psum(half, axis_two)
 
 
 def body(teacher_img, teacher_txt, student_img, student_txt):
@@ -50,7 +55,7 @@
         cols * txt_count
     )
     delta = (8.0 * (q_row - p_row + q_col - p_col)).astype(jnp.bfloat16)
-    loss = 0.5 * lax.psum(row_part + col_part, ("img", "txt"))
+    loss = 0.5 * one_after_other(row_part + col_part, "txt", "img")
     picked = delta
     grad_txt = lax.psum_scatter(
         scale_learn

time: 194 us -> 193 us (level)
  blocking collectives: 110 us -> 95.7 us
  waiting for transfers between devices: 27.5 us -> 40.7 us
    psum x1 -> x2, blocking collectives: 37.2 us -> 23.2 us  [the longest x1 14.2 us: one_after_other(): return lax.psum(half, axis_two)]
    reduce_scatter x1, waiting for transfers between devices: 27.5 us -> 38.8 us  [body(): lax.psum_scatter(scale_learn * jnp.einsum('ij,id->jd', picked, student_im...]
  transfers between devices with their start and end apart: 2 -> 2, of which waited for: 1 -> 2; matrix products, arithmetic and copies ran while one was open for 2% -> 2% of each run, Pallas kernels for 0% -> 0%
where the time goes in v1:
time: 193 us
  blocking collectives  95.7 us (50%)
  waiting for transfers between devices  40.7 us (21%)
  between operations  18.3 us (9%)
  other arithmetic  18.2 us (9%)
  matrix products  16.7 us (9%)
  local copies, waits for them, and re-layouts  3.03 us (2%)
    reduce_scatter x1, waiting for transfers between devices, body(): lax.psum_scatter(scale_learn * jnp.einsum('ij,id->jd', picked, student_im...  38.8 us
    psum x2, blocking collectives, body(): lax.psum((jnp.sum(jnp.exp(teacher - col_tpeak[None, :]), axis=0), jnp.sum...  27.2 us
    pmax x1, blocking collectives, body(): lax.pmax((jnp.max(teacher, axis=0), jnp.max(student, axis=0)), 'img')  18.3 us
    psum x2, blocking collectives, body(): lax.psum((jnp.sum(jnp.exp(teacher - row_tpeak[:, None]), axis=1), jnp.sum...  16.9 us
    psum x1, blocking collectives, one_after_other(): return lax.psum(half, axis_two)  14.2 us
    pmax x1, blocking collectives, body(): lax.pmax((jnp.max(teacher, axis=1), jnp.max(student, axis=1)), 'txt')  10.1 us
    psum x1, blocking collectives, one_after_other(): half = lax.psum(x, axis_one)  9 us
    reduce_sum x1, other arithmetic, body(): jnp.sum(p_col * gap) + jnp.sum(col_learn - col_teach) / img_count  8.12 us
  transfers between devices with their start and end apart: 2, of which 2 were waited for; matrix products, arithmetic and copies ran while one was open for 2% of the time, Pallas kernels for 0%

profile of v1, /device:TPU:0, one launch (start us, length us, event | category | flops | bytes accessed | tf_op | source)
XLA Modules:
  0.0 192.6 jit_solution(4732662656904826922)
XLA Ops:
  7.2 0.0 copy-start
  7.2 0.0 reduce-scatter.3.cloned.1.call-start
  7.2 1.7 copy-done
  8.9 0.0 copy-start.2
  8.9 0.0 copy-start.4
  8.9 6.4 %multiply_reduce_fusion.4 = (f32[1024]{0:T(1024)S(1)}, f32[1024]{0:T(1024)S(1)}, f32[1024,1024]{1,0:T(8,128)}) fusion(bf16[1024,1280]{1,0:T(8,128)(2,1)S(1)} %copy-done, bf16[1024,1280]{1,0:T(8,128)(2,1)} %param.5), kind=kOutput, calls=%fused_computation.12 | convolution fusion | flops 2687498240 | bytes 9445376 | tf_op jit(solution)/shard_map/id,jd->ij/dot_general | solution.py:20
  15.3 0.0 copy-done.2
  15.3 0.0 copy-done.4
  15.3 3.2 %multiply_reduce_fusion.2 = (f32[1024]{0:T(1024)S(1)}, f32[1024]{0:T(1024)S(1)}, f32[1024,1024]{1,0:T(8,128)}) fusion(bf16[1024,512]{1,0:T(8,128)(2,1)S(1)} %copy-done.4, bf16[1024,512]{1,0:T(8,128)(2,1)S(1)} %copy-done.2), kind=kOutput, calls=%fused_computation.9 | convolution fusion | flops 1076885504 | bytes 6299648 | tf_op jit(solution)/shard_map/id,jd->ij/dot_general | solution.py:23
  18.5 18.3 %all-reduce = (f32[1024]{0:T(1024)S(1)}, f32[1024]{0:T(1024)S(1)}) all-reduce(f32[1024]{0:T(1024)S(1)} %get-tuple-element.11, f32[1024]{0:T(1024)S(1)} %get-tuple-element.6), channel_id=1, replica_groups=mesh['img'=8,'txt'=4] {'img'}, use_global_device_ids=true, to_apply=%region_11.0 | all-reduce | flops 2048 | bytes 16384 | tf_op jit(solution)/shard_map/pmax | solution.py:27
  36.9 10.1 %all-reduce.1 = (f32[1024]{0:T(1024)S(1)}, f32[1024]{0:T(1024)S(1)}) all-reduce(f32[1024]{0:T(1024)S(1)} %get-tuple-element.12, f32[1024]{0:T(1024)S(1)} %get-tuple-element.7), channel_id=1, replica_groups=mesh['img'=8,'txt'=4] {'txt'}, use_global_device_ids=true, to_apply=%region_1.0 | all-reduce | flops 2048 | bytes 16384 | tf_op jit(solution)/shard_map/pmax | solution.py:26
  47.0 3.7 %exponential_reduce_fusion.1 = (f32[1024]{0:T(1024)S(1)}, f32[1024]{0:T(1024)S(1)}) fusion(f32[1024,1024]{1,0:T(8,128)} %get-tuple-element.21, f32[1024]{0:T(1024)S(1)} %get-tuple-element.13, f32[1024]{0:T(1024)S(1)} %get-tuple-element.15), kind=kLoop, calls=%fused_computation.4 | loop fusion | flops 5240832 | bytes 4210688 | tf_op jit(solution)/shard_map/reduce_sum | solution.py:37
  50.7 13.6 %psum.44 = f32[1024]{0:T(1024)S(1)} all-reduce(f32[1024]{0:T(1024)S(1)} %get-tuple-element.9), channel_id=1, replica_groups=mesh['img'=8,'txt'=4] {'img'}, use_global_device_ids=true, to_apply=%region_13.0 | all-reduce | flops 1024 | bytes 8192 | tf_op jit(solution)/shard_map/psum | solution.py:35
  64.3 7.9 %psum.42 = f32[1024]{0:T(1024)S(1)} all-reduce(f32[1024]{0:T(1024)S(1)} %get-tuple-element.10), channel_id=1, replica_groups=mesh['img'=8,'txt'=4] {'txt'}, use_global_device_ids=true, to_apply=%region_3.0 | all-reduce | flops 1024 | bytes 8192 | tf_op jit(solution)/shard_map/psum | solution.py:28
  72.2 8.1 %multiply_reduce_fusion = (f32[]{:T(128)}, f32[]{:T(128)}, f32[1024]{0:T(1024)S(1)}, f32[1024]{0:T(1024)S(1)}) fusion(f32[1024,1024]{1,0:T(8,128)} %get-tuple-element.22, f32[1024,1024]{1,0:T(8,128)} %get-tuple-element.21, f32[1024]{0:T(1024)S(1)} %log_add_fusion.1, f32[1024]{0:T(1024)S(1)} %log_add_fusion.3, f32[1024]{0:T(1024)S(1)} %get-tuple-element.14, ...), kind=kLoop, calls=%fused_computation.2 | loop fusion | flops 13629438 | bytes 8413192 | tf_op jit(solution)/shard_map/reduce_sum | solution.py:54
  80.4 13.6 %psum.45 = f32[1024]{0:T(1024)S(1)} all-reduce(f32[1024]{0:T(1024)S(1)} %get-tuple-element.5), channel_id=1, replica_groups=mesh['img'=8,'txt'=4] {'img'}, use_global_device_ids=true, to_apply=%region_18.0 | all-reduce | flops 1024 | bytes 8192 | tf_op jit(solution)/shard_map/psum | solution.py:35
  93.9 0.6 subtract_reduce_fusion
  94.5 9.0 %psum.43 = f32[1024]{0:T(1024)S(1)} all-reduce(f32[1024]{0:T(1024)S(1)} %get-tuple-element.8), channel_id=1, replica_groups=mesh['img'=8,'txt'=4] {'txt'}, use_global_device_ids=true, to_apply=%region_8.0 | all-reduce | flops 1024 | bytes 8192 | tf_op jit(solution)/shard_map/psum | solution.py:28
  103.5 0.6 subtract_reduce_fusion.1
  104.2 5.1 %multiply_convert_fusion = bf16[1024,1024]{1,0:T(8,128)(2,1)S(1)} fusion(f32[1024,1024]{1,0:T(8,128)} %get-tuple-element.22, f32[1024,1024]{1,0:T(8,128)} %get-tuple-element.21, f32[1024]{0:T(1024)S(1)} %get-tuple-element.18, f32[1024]{0:T(1024)S(1)} %get-tuple-element.20, f32[1024]{0:T(1024)S(1)} %log_add_fusion.1, f32[1024]{0:T(1024)S(1)} %log_add_fusion.3), kind=kLoop, calls=%fused_computation | loop fusion | flops 11534336 | bytes 10502144 | tf_op jit(solution)/shard_map/convert_element_type | solution.py:57
  109.2 0.0 copy-start.1
  109.2 1.3 copy-done.1
  110.6 0.0 copy-done.3
  110.6 2.6 %convolution_multiply_fusion.1 = f32[1024,512]{1,0:T(8,128)} fusion(bf16[1024,1024]{1,0:T(8,128)(2,1)S(1)} %multiply_convert_fusion, bf16[1024,512]{1,0:T(8,128)(2,1)S(1)} %copy-done.3), kind=kOutput, calls=%fused_computation.15 | convolution fusion | flops 1074266112 | bytes 5242880 | tf_op jit(solution)/shard_map/dot_general | solution.py:69
  113.2 0.0 reduce-scatter.3.cloned.1.call-update
  113.2 0.0 reduce-scatter.5.cloned.1.call-start
  113.2 4.4 %convolution_multiply_fusion = f32[1024,512]{1,0:T(8,128)} fusion(bf16[1024,1024]{1,0:T(8,128)(2,1)} %copy-done.1, bf16[1024,512]{1,0:T(8,128)(2,1)} %param.6), kind=kOutput, calls=%fused_computation.14 | convolution fusion | flops 1074266112 | bytes 5242880 | tf_op jit(solution)/shard_map/ij,id->jd/dot_general | solution.py:62
  117.7 0.0 reduce-scatter.5.cloned.1.call-update
  120.1 9.0 %psum.46 = f32[]{:T(128)} all-reduce(f32[]{:T(128)S(6)} %add.46), channel_id=1, replica_groups=mesh['img'=8,'txt'=4] {'txt'}, use_global_device_ids=true, to_apply=%region_20.0 | all-reduce | flops 1 | bytes 8 | tf_op jit(solution)/shard_map/psum | solution.py:9
  129.1 14.2 %psum.47 = f32[]{:T(128)} all-reduce(f32[]{:T(128)} %psum.46), channel_id=1, replica_groups=mesh['img'=8,'txt'=4] {'img'}, use_global_device_ids=true, to_apply=%region_21.0 | all-reduce | flops 1 | bytes 8 | tf_op jit(solution)/shard_map/psum | solution.py:10
  144.0 1.9 reduce-scatter.3.cloned.1.call-done
  145.9 38.8 %reduce-scatter.5.cloned.1.call-done = f32[128,512]{1,0:T(8,128)} async-done(((f32[1024,512]{1,0:T(8,128)}), f32[128,512]{1,0:T(8,128)}) %reduce-scatter.5.cloned.1.call-update) | async-done | bytes 262160 | tf_op jit(solution)/shard_map/reduce_scatter | solution.py:60
  (3 shorter events, 0.0 us)
Async XLA Ops:
  7.2 1.7 copy-start
  7.2 138.7 %reduce-scatter.3.cloned.1.call-start = ((), (), s32[]{:S(2)}) async-start(), calls=%async_computation.2 | async-start | bytes 2621440 | tf_op jit(solution)/shard_map/reduce_scatter | solution.py:68
  8.9 6.4 %copy-start.2 = (bf16[1024,512]{1,0:T(8,128)(2,1)S(1)}, bf16[1024,512]{1,0:T(8,128)(2,1)}, u32[]{:S(2)}) copy-start(bf16[1024,512]{1,0:T(8,128)(2,1)} %param.7) | copy-start | bytes 3145732
  8.9 6.4 %copy-start.4 = (bf16[1024,512]{1,0:T(8,128)(2,1)S(1)}, bf16[1024,512]{1,0:T(8,128)(2,1)}, u32[]{:S(2)}) copy-start(bf16[1024,512]{1,0:T(8,128)(2,1)} %param.6) | copy-start | bytes 3145732
  104.2 6.4 %copy-start.3 = (bf16[1024,512]{1,0:T(8,128)(2,1)S(1)}, bf16[1024,512]{1,0:T(8,128)(2,1)}, u32[]{:S(2)}) copy-start(bf16[1024,512]{1,0:T(8,128)(2,1)} %param.7) | copy-start | bytes 3145732
  109.2 1.3 copy-start.1
  113.2 71.5 %reduce-scatter.5.cloned.1.call-start = ((), (), s32[]{:S(2)}) async-start(), calls=%async_computation.3 | async-start | bytes 2359296 | tf_op jit(solution)/shard_map/reduce_scatter | solution.py:60
Sparse Core Ops, SparseCore 0:
  113.3 32.5 reduce-scatter.2
  148.7 35.8 reduce-scatter.4
